TPU v7x, 128 devices: a whole 4x4x4 slice. The times are simulated.
128 devices in a mesh: layer: 8 (over x_lo, z), feat: 16 (over y, x_hi, core).
Axes of the slice: x: 4 (x_hi: 2, x_lo: 2; x = x_hi * 2 + x_lo), y: 4, z: 4, core: 2. Of those that a mesh axis runs over, the one named last changes fastest.
Arguments:
- sources: bfloat16 [8, 1024, 2304], P('layer', 'feat'), may hold values from -6 to 6
- w_encode: bfloat16 [8, 2304, 16384], P('layer', None, 'feat'), may hold values from -0.125 to 0.125
- b_encode: float32 [8, 16384], P('layer', 'feat'), may hold values from -3 to 3
- w_decode: bfloat16 [8, 16384, 2304], P('layer', 'feat'), may hold values from -0.046875 to 0.046875
- b_decode: float32 [2304], replicated, may hold values from -3 to 3
- target: bfloat16 [1024, 2304], replicated, may hold values from -6 to 6
Outputs:
- error: float32 [1024, 2304], P(('layer', 'feat'))
- feature_grad: bfloat16 [8, 1024, 16384], P('layer', None, 'feat')
- decoder_grad: bfloat16 [8, 16384, 2304], P('layer', 'feat')
All inputs are finite; a program needn't handle non-finite values.
Results may differ from a plain program's by a relative error of at most 0.0056.
Values may be sent and summed in bfloat16 or wider, within the bound.
No kernel may reach another device: no remote copies, remote signals or barrier semaphores. Data moves between devices by JAX's collectives and lax.ppermute only.
A program may use at most 128 MiB of HBM per device.

v0:
```python
import math

import jax
import jax.numpy as jnp
from jax import lax
from jax.sharding import PartitionSpec as P


def body(sources, w_encode, b_encode, w_decode, b_decode, target):
    encoder = w_encode[0]
    bias = b_encode[0]
    decoder = w_decode[0]
    pre = (
        jnp.dot(
            lax.all_gather(sources[0], "feat", axis=0, tiled=True),
            encoder,
            preferred_element_type=jnp.float32,
        )
        + bias
    )
    acts = jnp.maximum(pre, 0.0).astype(jnp.bfloat16)
    tokens = acts.shape[0]
    scale = 1.0 / math.sqrt(tokens)
    groups = lax.axis_size("layer") * lax.axis_size("feat")
    rows_dev = tokens // groups
    own = lax.axis_index("layer") * lax.axis_size("feat") + lax.axis_index("feat")
    total = lax.psum(jnp.dot(acts, decoder, preferred_element_type=jnp.float32), ("layer", "feat"))
    error_full = total + b_decode - target.astype(jnp.float32)
    error_low = error_full.astype(jnp.bfloat16)
    error_out = lax.dynamic_slice_in_dim(error_full, own * rows_dev, rows_dev, 0)
    grad_feat = lax.dot_general(
        error_low, decoder, (((1,), (1,)), ((), ())), preferred_element_type=jnp.float32
    )
    grad_dec = lax.dot_general(
        acts, error_low, (((0,), (0,)), ((), ())), preferred_element_type=jnp.float32
    )
    feature_grad = grad_feat.astype(jnp.bfloat16)[None]
    decoder_grad = (grad_dec * scale).astype(jnp.bfloat16)[None]
    return (error_out, feature_grad, decoder_grad)


def solution(mesh):
    placed = (
        P("layer", "feat", None),
        P("layer", None, "feat"),
        P("layer", "feat"),
        P("layer", "feat", None),
        P(),
        P(),
    )
    return jax.shard_map(
        body,
        mesh=mesh,
        in_specs=placed,
        out_specs=(P(("layer", "feat"), None), P("layer", None, "feat"), P("layer", "feat", None)),
        check_vma=False,
    )
```

profile of v0, /device:TPU:1, one launch (start us, length us, event | category | flops | bytes accessed | tf_op | source)
XLA Modules:
  0.0 278.8 jit_solution(17509943103213933336)
XLA Ops:
  7.2 0.0 all-gather.3.cloned.1.call-start
  7.2 0.7 all-gather.3.cloned.1.call-update
  7.9 0.0 all-reduce.2.cloned.1.call-start
  7.9 63.0 %all-gather.3.cloned.1.call-done = bf16[1,1024,2304]{2,1,0:T(8,128)(2,1)} async-done(((bf16[1,64,2304]{2,1,0:T(8,128)(2,1)}), bf16[1,1024,2304]{2,1,0:T(8,128)(2,1)}) %all-gather.3.cloned.1.call-update) | async-done | bytes 4718608 | tf_op jit(solution)/shard_map/all_gather | solution.py:15
  70.9 0.0 copy-start.1
  70.9 8.5 %maximum_convert_fusion = bf16[1024,1024]{1,0:T(8,128)(2,1)S(1)} fusion(f32[1024]{0:T(1024)} %bitcast.24, bf16[1,2304,1024]{2,1,0:T(8,128)(2,1)} %param.7, bf16[1,1024,2304]{2,1,0:T(8,128)(2,1)} %all-gather.3.cloned.1.call-done), kind=kOutput, calls=%fused_computation.10 | convolution fusion | flops 4834983936 | bytes 11538432 | tf_op jit(solution)/shard_map/dot_general | solution.py:14
  79.4 0.0 copy-start.2
  79.4 1.3 copy-done.2
  80.7 0.0 copy-done.1
  80.7 7.3 %fusion.3 = f32[1024,2304]{1,0:T(8,128)} fusion(bf16[1024,1024]{1,0:T(8,128)(2,1)S(1)} %maximum_convert_fusion, bf16[1,1024,2304]{2,1,0:T(8,128)(2,1)S(1)} %copy-done.1), kind=kOutput, calls=%fused_computation.5 | convolution fusion | flops 4831838208 | bytes 16252928 | tf_op jit(solution)/shard_map/dot_general | solution.py:27
  88.0 0.0 copy-start
  88.0 0.0 all-reduce.2.cloned.1.call-update
  88.1 161.3 %all-reduce.2.cloned.1.call-done = f32[1024,2304]{1,0:T(8,128)} async-done(((f32[1024,2304]{1,0:T(8,128)}), f32[1024,2304]{1,0:T(8,128)}) %all-reduce.2.cloned.1.call-update) | async-done | bytes 9437200 | tf_op jit(solution)/shard_map/psum | solution.py:27
  249.4 0.0 copy-done
  249.4 6.0 %convert_subtract_fusion = f32[1024,2304]{1,0:T(8,128)S(1)} fusion(bf16[1024,2304]{1,0:T(8,128)(2,1)} %param.11, f32[1024,2304]{1,0:T(8,128)} %all-reduce.2.cloned.1.call-done, f32[2304]{0:T(1024)S(1)} %copy-done), kind=kLoop, calls=%fused_computation.1 | loop fusion | flops 7077888 | bytes 23602176 | tf_op jit(solution)/shard_map/sub | solution.py:28
  255.5 0.0 copy-start.3
  255.5 8.8 %convert_bitcast_fusion = bf16[1,1024,1024]{2,1,0:T(8,128)(2,1)} fusion(bf16[1,1024,2304]{2,1,0:T(8,128)(2,1)} %param.9, f32[1024,2304]{1,0:T(8,128)S(1)} %convert_subtract_fusion), kind=kOutput, calls=%fused_computation.13 | convolution fusion | flops 4835246080 | bytes 16252928 | tf_op jit(solution)/shard_map/dot_general | solution.py:31
  264.3 0.0 copy-done.3
  264.3 7.1 %fusion = bf16[1,1024,2304]{2,1,0:T(8,128)(2,1)} fusion(bf16[1024,1024]{1,0:T(8,128)(2,1)S(1)} %copy-done.3, f32[1024,2304]{1,0:T(8,128)S(1)} %convert_subtract_fusion), kind=kOutput, calls=%fused_computation.2 | convolution fusion | flops 4838916096 | bytes 16252928 | tf_op jit(solution)/shard_map/dot_general | solution.py:34
  271.4 0.6 constant_dynamic-slice_fusion
Async XLA Ops:
  7.2 63.7 %all-gather.3.cloned.1.call-start = ((), (), s32[]{:S(2)}) async-start(), calls=%async_computation.1 | async-start | bytes 5013504 | tf_op jit(solution)/shard_map/all_gather | solution.py:15
  7.9 241.5 %all-reduce.2.cloned.1.call-start = ((), (), s32[]{:S(2)}) async-start(), calls=%async_computation | async-start | bytes 18874368 | tf_op jit(solution)/shard_map/psum | solution.py:27
  70.9 9.8 %copy-start.1 = (bf16[1,1024,2304]{2,1,0:T(8,128)(2,1)S(1)}, bf16[1,1024,2304]{2,1,0:T(8,128)(2,1)}, u32[]{:S(2)}) copy-start(bf16[1,1024,2304]{2,1,0:T(8,128)(2,1)} %param.9) | copy-start | bytes 14155780
  79.4 1.3 copy-start.2
  88.0 161.4 %copy-start = (f32[2304]{0:T(1024)S(1)}, f32[2304]{0:T(1024)}, u32[]{:S(2)}) copy-start(f32[2304]{0:T(1024)} %param.10) | copy-start | bytes 27652
  255.5 8.8 %copy-start.3 = (bf16[1024,1024]{1,0:T(8,128)(2,1)S(1)}, bf16[1024,1024]{1,0:T(8,128)(2,1)}, u32[]{:S(2)}) copy-start(bf16[1024,1024]{1,0:T(8,128)(2,1)} %copy-done.2) | copy-start | bytes 6291460
Sparse Core Ops, SparseCore 0:
  10.4 60.4 all-gather.2
  88.2 161.1 all-reduce.1
where the time goes:
time: 279 us
  waiting for transfers between devices  225 us (81%)
  matrix products  31.7 us (11%)
  between operations  14.1 us (5%)
  other arithmetic  6.04 us (2%)
    psum x1, waiting for transfers between devices, body(): lax.psum(jnp.dot(acts, decoder, preferred_element_type=jnp.float32), ('la...  161 us
    all_gather x1, waiting for transfers between devices, body(): lax.all_gather(sources[0], 'feat', axis=0, tiled=True)  63 us
    dot_general x1, matrix products, body(): lax.dot_general(error_low, decoder, (((1,), (1,)), ((), ())), preferred_e...  8.79 us
    dot_general x1, matrix products, body(): jnp.dot(lax.all_gather(sources[0], 'feat', axis=0, tiled=True), encoder,...  8.46 us
    dot_general x1, matrix products, body(): jnp.dot(acts, decoder, preferred_element_type=jnp.float32)  7.35 us
    dot_general x1, matrix products, body(): lax.dot_general(acts, error_low, (((0,), (0,)), ((), ())), preferred_elem...  7.1 us
    sub x1, other arithmetic, body(): error_full = total + b_decode - target.astype(jnp.float32)  6.04 us
  transfers between devices with their start and end apart: 2, of which 2 were waited for; matrix products, arithmetic and copies ran while one was open for 0% of the time, Pallas kernels for 0%

commit v1 on v0

v1 whole, which is shorter than its diff:
```python
import math

import jax
import jax.numpy as jnp
from jax import lax
from jax.experimental import pallas as pl
from jax.experimental.pallas import tpu as pltpu
from jax.sharding import Mesh
from jax.sharding import PartitionSpec as P


AXES = ("xl", "z", "y", "xh", "c")
LAYER = ("xl", "z")
FEAT = ("y", "xh", "c")
DEVICES = [
    (xl, z, y, xh, c)
    for xl in range(2)
    for z in range(4)
    for y in range(4)
    for xh in range(2)
    for c in range(2)
]


def index(xl, z, y, xh, c):
    return (((xl * 4 + z) * 4 + y) * 2 + xh) * 2 + c


def pairs(to):
    return [(index(*d), index(*to(*d))) for d in DEVICES]


def move(value, to):
    return lax.ppermute(value, AXES, pairs(to))


def by_y(k):
    return lambda xl, z, y, xh, c: (xl, z, y ^ k, xh, c)


def by_x(k):
    return lambda xl, z, y, xh, c: (xl ^ (k & 1), z, y, xh ^ (k >> 1), c)


def by_z(k):
    return lambda xl, z, y, xh, c: (xl, z ^ k, y, xh, c)


def by_xh(xl, z, y, xh, c):
    return (xl, z, y, xh ^ 1, c)


def by_core(xl, z, y, xh, c):
    return (xl, z, y, xh, c ^ 1)


def first(k):
    return lambda xl, z, y, xh, c: (by_y(k) if c == 0 else by_x(k))(xl, z, y, xh, c)


def second(k):
    return lambda xl, z, y, xh, c: (by_x(k) if c == 0 else by_y(k))(xl, z, y, xh, c)


def owner(xl, z, y, xh, c):
    return (y >> 1, ((y & 1) << 1) | xh, (c << 1) | xl, z >> 1, z & 1)


SPANS = ((0, 1280), (1280, 2304))
MIB = 1024 * 1024
VMEM = pl.BlockSpec(memory_space=pltpu.VMEM)
HBM = pl.BlockSpec(memory_space=pltpu.HBM)


def call(kernel, args, outs, *, limit, flops=0, moved=0, specs=None, scratch=()):
    return pl.pallas_call(
        kernel,
        in_specs=specs or [VMEM] * len(args),
        out_specs=[VMEM] * len(outs),
        out_shape=[jax.ShapeDtypeStruct(shape, dtype) for shape, dtype in outs],
        scratch_shapes=list(scratch),
        compiler_params=pltpu.CompilerParams(vmem_limit_bytes=limit * MIB),
        cost_estimate=pl.CostEstimate(
            flops=int(flops), bytes_accessed=int(moved), transcendentals=0
        ),
    )(*args)


def prefetch(*arrays):
    def kernel(*refs):
        count = len(arrays)
        ins, outs, sems = refs[:count], refs[count : 2 * count], refs[2 * count]
        copies = [pltpu.make_async_copy(ins[i], outs[i], sems.at[i]) for i in range(count)]
        for copy in copies:
            copy.start()
        for copy in copies:
            copy.wait()

    return call(
        kernel,
        arrays,
        [(a.shape, a.dtype) for a in arrays],
        limit=12,
        moved=sum(a.size * a.dtype.itemsize for a in arrays),
        specs=[HBM] * len(arrays),
        scratch=[pltpu.SemaphoreType.DMA((len(arrays),))],
    )


def encode(pieces, weight, bias):
    rows, depth = pieces[0].shape
    width = weight.shape[1]
    tile = 512
    total = rows * len(pieces)

    def kernel(*refs):
        parts, (w_ref, b_ref, out_ref, x_ref) = refs[: len(pieces)], refs[len(pieces) :]
        for i, part in enumerate(parts):
            x_ref[i * rows : (i + 1) * rows, :] = part[...]
        for j in range(0, width, tile):
            cols = slice(j, j + tile)
            pre = jnp.dot(x_ref[...], w_ref[:, cols], preferred_element_type=jnp.float32)
            out_ref[:, cols] = jnp.maximum(pre + b_ref[:, cols], 0.0).astype(jnp.bfloat16)

    (out,) = call(
        kernel,
        (*pieces, weight, bias),
        [((total, width), jnp.bfloat16)],
        limit=20,
        flops=2 * total * depth * width,
        moved=2 * total * depth,
        scratch=[pltpu.VMEM((total, depth), jnp.bfloat16)],
    )
    return out


def decode(acts, weight, spans):
    rows, feats = acts.shape
    half = rows // 2
    tile = 256

    def kernel(a_ref, w_ref, *outs):
        for i, (begin, end) in enumerate(spans):
            for j in range(begin, end, tile):
                cols = slice(j - begin, j - begin + tile)
                out = jnp.dot(
                    a_ref[...], w_ref[:, j : j + tile], preferred_element_type=jnp.float32
                )
                outs[2 * i][:, cols] = out[:half, :]
                outs[2 * i + 1][:, cols] = out[half:, :].astype(jnp.bfloat16)

    shapes = []
    for begin, end in spans:
        shapes += [((half, end - begin), jnp.float32), ((half, end - begin), jnp.bfloat16)]
    total = sum(end - begin for begin, end in spans)
    return call(
        kernel,
        (acts, weight),
        shapes,
        limit=20,
        flops=2 * rows * feats * total,
        moved=6 * half * total,
    )


def split_cores(keeps, gots):
    width = keeps[0].shape[1]
    rows = 128

    def kernel(k0, k1, g0, g1, *outs):
        keep, got = (k0, k1), (g0, g1)
        core, xl = lax.axis_index("c"), lax.axis_index("xl")
        for flip in range(2):

            @pl.when(core == flip)
            def _(flip=flip):
                for a in range(4):
                    for b in range(4):
                        dy, dx = (b, a) if flip else (a, b)
                        at = pl.multiple_of((dy * 2 + ((dx & 1) ^ xl)) * 32, 32)
                        src = (pl.ds(at, 32), slice(None))
                        value = keep[dx >> 1][src] + got[dx >> 1][src].astype(jnp.float32)
                        outs[a][b * 32 : b * 32 + 32, :] = value.astype(outs[a].dtype)

    return call(
        kernel,
        (*keeps, *gots),
        [((rows, width), jnp.float32)] + [((rows, width), jnp.bfloat16)] * 3,
        limit=12,
        flops=512 * width,
        moved=512 * width * 9,
    )


def split_first(owns, gots):
    rows = owns[0].shape[0]
    part = rows // 4
    depth = SPANS[-1][1]

    def kernel(*refs):
        ins, outs = refs[: 4 * len(SPANS)], refs[4 * len(SPANS) :]
        for i, (begin, end) in enumerate(SPANS):
            own, *others = ins[4 * i : 4 * i + 4]
            for b, out in enumerate(outs):
                src = slice(b * part, (b + 1) * part)
                value = own[src, :]
                for got in others:
                    value = value + got[src, :].astype(jnp.float32)
                out[:, begin:end] = value.astype(out.dtype)

    args = []
    for own, got in zip(owns, gots):
        args += [own, *got]
    return call(
        kernel,
        args,
        [((part, depth), jnp.float32)] + [((part, depth), jnp.bfloat16)] * 3,
        limit=8,
        flops=4 * rows * depth,
        moved=rows * depth * 12,
    )


def add(own, gots):
    def kernel(own_ref, g1, g2, g3, out, low):
        value = own_ref[...]
        for got in (g1, g2, g3):
            value = value + got[...].astype(jnp.float32)
        out[...] = value
        low[...] = value.astype(jnp.bfloat16)

    return call(
        kernel,
        (own, *gots),
        [(own.shape, jnp.float32), (own.shape, jnp.bfloat16)],
        limit=4,
        flops=3 * own.size,
        moved=own.size * 16,
    )


def finish(own, gots, target, bias):
    rows, depth = own.shape

    def kernel(own_ref, g1, g2, g3, t_hbm, b_hbm, rows_ref, low_ref, t_ref, b_ref, err_ref, sems):
        y, xh, c, xl, z = (lax.axis_index(name) for name in ("y", "xh", "c", "xl", "z"))
        at = pl.multiple_of((((y * 2 + xh) * 2 + c) * 2 + xl) * rows, rows)
        one = pltpu.make_async_copy(t_hbm.at[pl.ds(at, rows), :], t_ref, sems.at[0])
        two = pltpu.make_async_copy(b_hbm, b_ref, sems.at[1])
        one.start()
        two.start()
        value = own_ref[...]
        for got in (g1, g2, g3):
            value = value + got[...].astype(jnp.float32)
        one.wait()
        two.wait()
        value = value + b_ref[...] - t_ref[...].astype(jnp.float32)
        err_ref[...] = value
        low_ref[...] = value.astype(jnp.bfloat16)
        rows_ref[...] = err_ref[pl.ds(pl.multiple_of(z * 8, 8), 8), :]

    return call(
        kernel,
        (own, *gots, target, bias),
        [((8, depth), jnp.float32), ((rows, depth), jnp.bfloat16)],
        limit=4,
        flops=6 * own.size,
        moved=own.size * 16,
        specs=[VMEM] * 4 + [HBM] * 2,
        scratch=[
            pltpu.VMEM((rows, depth), jnp.bfloat16),
            pltpu.VMEM((1, depth), jnp.float32),
            pltpu.VMEM((rows, depth), jnp.float32),
            pltpu.SemaphoreType.DMA((2,)),
        ],
    )


def join(pieces):
    rows = pieces[0].shape[0]

    def kernel(*refs):
        ins, outs = refs[: len(pieces)], refs[len(pieces) :]
        for (begin, end), out in zip(SPANS, outs):
            for i, piece in enumerate(ins):
                out[i * rows : (i + 1) * rows, :] = piece[:, begin:end]

    return call(
        kernel,
        pieces,
        [((rows * len(pieces), end - begin), jnp.bfloat16) for begin, end in SPANS],
        limit=4,
        moved=4 * sum(p.size for p in pieces),
    )


def gradients(mine, theirs, acts, decoder, scale, span, partial, made):
    feats, depth = decoder.shape
    begin, end = SPANS[span]
    width = end - begin
    tokens = 1024
    tile = 256
    steps = feats // tile
    last = span == len(SPANS) - 1
    begun = span > 0

    def kernel(*refs):
        parts, (a0, a1, w_ref), refs = refs[:8], refs[8:11], list(refs[11:])
        part_ref = refs.pop(0) if begun else None
        if begun:
            refs.pop(0)
        fg_ref, dg_ref, e_ref, x_ref, dg_tile, sems = refs
        y, xh, c, xl = (lax.axis_index(name) for name in ("y", "xh", "c", "xl"))

        def row(dy, dh, dc, j5):
            where = ((((y ^ dy) * 2 + (xh ^ dh)) * 2 + (c ^ dc)) * 2 + j5) * 32
            return pl.ds(pl.multiple_of(where, 32), 32)

        for flip in range(2):

            @pl.when(c == flip)
            def _(flip=flip):
                for dc in range(2):
                    for a in range(4):
                        for b in range(4):
                            dy, dx = (b, a) if flip ^ dc else (a, b)
                            e_ref[row(dy, dx >> 1, dc, xl ^ (dx & 1)), :] = parts[dc * 4 + a][
                                b * 32 : b * 32 + 32, :
                            ]

        for dh, act in enumerate((a0, a1)):
            for dc in range(2):
                for dy in range(4):
                    src = (dc * 4 + dy) * 64
                    where = (((y ^ dy) * 2 + (xh ^ dh)) * 2 + (c ^ dc)) * 64
                    x_ref[pl.ds(pl.multiple_of(where, 64), 64), :] = act[src : src + 64, :]
        error = e_ref[...]

        def out_copy(i):
            return pltpu.make_async_copy(
                dg_tile.at[i % 2],
                dg_ref.at[i * tile : (i + 1) * tile, begin:end],
                sems.at[i % 2],
            )

        for i in range(steps):
            cols = slice(i * tile, (i + 1) * tile)
            fg = lax.dot_general(
                error,
                w_ref[cols, begin:end],
                (((1,), (1,)), ((), ())),
                preferred_element_type=jnp.float32,
            )
            if begun:
                fg = fg + part_ref[:, cols]
            fg_ref[:, cols] = fg.astype(fg_ref.dtype)
            if i >= 2:
                out_copy(i - 2).wait()
            dg_tile[i % 2] = (
                lax.dot_general(
                    x_ref[:, cols],
                    error,
                    (((0,), (0,)), ((), ())),
                    preferred_element_type=jnp.float32,
                )
                * scale
            ).astype(jnp.bfloat16)
            out_copy(i).start()
        for i in range(steps - 2, steps):
            out_copy(i).wait()

    extra = [partial, made] if begun else []
    return pl.pallas_call(
        kernel,
        in_specs=[VMEM] * 11 + ([VMEM, HBM] if begun else []),
        out_specs=[VMEM, HBM],
        out_shape=[
            jax.ShapeDtypeStruct((tokens, feats), jnp.bfloat16 if last else jnp.float32),
            jax.ShapeDtypeStruct((feats, depth), jnp.bfloat16),
        ],
        input_output_aliases={12: 1} if begun else {},
        scratch_shapes=[
            pltpu.VMEM((tokens, width), jnp.bfloat16),
            pltpu.VMEM((tokens, feats), jnp.bfloat16),
            pltpu.VMEM((2, tile, width), jnp.bfloat16),
            pltpu.SemaphoreType.DMA((2,)),
        ],
        compiler_params=pltpu.CompilerParams(vmem_limit_bytes=32 * MIB),
        cost_estimate=pl.CostEstimate(
            flops=4 * tokens * feats * width,
            bytes_accessed=2 * (tokens * width + 2 * feats * width + 4 * tokens * feats),
            transcendentals=0,
        ),
        name="gradients",
    )(*mine, *theirs, *acts, decoder, *extra)


def body(sources, w_encode, b_encode, w_decode, b_decode, target):
    scale = 1.0 / math.sqrt(target.shape[0])
    block = sources[0]
    encoder, bias, decoder, own_block = prefetch(w_encode[0], b_encode, w_decode[0], block)

    across = move(block, by_xh)
    near = [own_block] + [move(block, by_y(k)) for k in (1, 2, 3)]
    far = [across, move(across, by_y(1)), move(near[2], by_xh), move(across, by_y(3))]

    near_acts = encode(near + [move(piece, by_core) for piece in near], encoder, bias)
    *far, near_acts = lax.optimization_barrier((*far, near_acts))
    keep_a, send_a, keep_b, send_b = decode(near_acts, decoder, SPANS)
    keeps, gots = [[keep_a], [keep_b]], [[move(send_a, by_core)], [move(send_b, by_core)]]
    far_acts = encode(far + [move(piece, by_core) for piece in far], encoder, bias)
    owns, firsts = [], []
    for span in range(len(SPANS)):
        keep, send = decode(far_acts, decoder, SPANS[span : span + 1])
        keeps[span].append(keep)
        gots[span].append(move(send, by_core))
    for span in range(len(SPANS)):
        own, *sends = split_cores(keeps[span], gots[span])
        owns.append(own)
        firsts.append([move(send, first(k + 1)) for k, send in enumerate(sends)])
    own, *sends = split_first(owns, firsts)
    own, low = add(own, [move(send, second(k + 1)) for k, send in enumerate(sends)])
    rows, low = finish(own, [move(low, by_z(k)) for k in (1, 2, 3)], target, b_decode[None])

    lows = join([low] + [move(low, second(k)) for k in (1, 2, 3)])
    feature_grad = decoder_grad = None
    acts = (near_acts, far_acts)
    for span, low in enumerate(lows):
        mine = [low] + [move(low, first(k)) for k in (1, 2, 3)]
        if span == len(lows) - 1:
            *mine, feature_grad = lax.optimization_barrier((*mine, feature_grad))
        theirs = [move(piece, by_core) for piece in mine]
        feature_grad, decoder_grad = gradients(
            mine, theirs, acts, decoder, scale, span, feature_grad, decoder_grad
        )
    rows = move(rows, owner)
    return rows, feature_grad[None], decoder_grad[None]


def solution(mesh):
    grid = Mesh(mesh.devices.reshape(2, 4, 4, 2, 2), AXES)
    return jax.shard_map(
        body,
        mesh=grid,
        in_specs=(
            P(LAYER, FEAT, None),
            P(LAYER, None, FEAT),
            P(LAYER, FEAT),
            P(LAYER, FEAT, None),
            P(),
            P(),
        ),
        out_specs=(P(AXES, None), P(LAYER, None, FEAT), P(LAYER, FEAT, None)),
        check_vma=False,
    )
```

time: 279 us -> 144 us (0.52)
  the two profiles are of different devices: /device:TPU:1 before, /device:TPU:6 now
where the time goes in v1:
time: 144 us
  waiting for transfers between devices  59.3 us (41%)
  starting transfers between devices  46.7 us (32%)
  Pallas kernels  29.9 us (21%)
  local copies, waits for them, and re-layouts  6.98 us (5%)
    ppermute x49, waiting for transfers between devices, move(): return lax.ppermute(value, AXES, pairs(to))  59.3 us
    ppermute x49, starting transfers between devices, move(): return lax.ppermute(value, AXES, pairs(to))  46.7 us
    pallas_call x2, Pallas kernels, gradients(): pl.pallas_call(kernel, in_specs=[VMEM] * 11 + ([VMEM, HBM] if begun else...  17.2 us
    pallas_call x12, Pallas kernels, call(): pl.pallas_call(kernel, in_specs=specs or [VMEM] * len(args), out_specs=[V...  12.7 us
    unnamed x15, local copies, waits for them, and re-layouts  6.97 us
  transfers between devices with their start and end apart: 49, of which 17 were waited for; matrix products, arithmetic and copies ran while one was open for 0% of the time, Pallas kernels for 14%

profile of v1, /device:TPU:6, one launch (start us, length us, event | category | flops | bytes accessed | tf_op | source)
XLA Modules:
  0.0 143.8 jit_solution(12573367221826922930)
XLA Ops:
  0.6 3.1 %collective-permute-start.6 = (bf16[64,2304]{1,0:T(8,128)(2,1)}, bf16[64,2304]{1,0:T(8,128)(2,1)S(1)}, u32[]{:S(2)}, u32[]{:S(2)}) collective-permute-start(bf16[64,2304]{1,0:T(8,128)(2,1)} %bitcast.9), channel_id=1, source_target_pairs={{0,12},{1,13},{2,14},{3,15},{4,8},{5,9},{6,10},{7,11},{8,4},{9,5},... | collective-permute-start | bytes 884744 | tf_op jit(solution)/shard_map/ppermute | solution.py:34
  3.9 1.5 %collective-permute-start.2 = (bf16[64,2304]{1,0:T(8,128)(2,1)}, bf16[64,2304]{1,0:T(8,128)(2,1)S(1)}, u32[]{:S(2)}, u32[]{:S(2)}) collective-permute-start(bf16[64,2304]{1,0:T(8,128)(2,1)} %bitcast.11), channel_id=1, source_target_pairs={{0,8},{1,9},{2,10},{3,11},{4,12},{5,13},{6,14},{7,15},{8,0},{9,1},... | collective-permute-start | bytes 884744 | tf_op jit(solution)/shard_map/ppermute | solution.py:34
  6.8 2.3 %copy-done = bf16[1,2304,1024]{2,1,0:T(8,128)(2,1)S(1)} copy-done((bf16[1,2304,1024]{2,1,0:T(8,128)(2,1)S(1)}, bf16[1,2304,1024]{2,1,0:T(8,128)(2,1)}, u32[]{:S(2)}) %copy-start) | copy-done | bytes 4718616
  9.2 2.3 %copy-done.1 = bf16[1,1024,2304]{2,1,0:T(8,128)(2,1)S(1)} copy-done((bf16[1,1024,2304]{2,1,0:T(8,128)(2,1)S(1)}, bf16[1,1024,2304]{2,1,0:T(8,128)(2,1)}, u32[]{:S(2)}) %copy-start.1) | copy-done | bytes 4718616
  14.6 4.0 %collective-permute-done.2.refs_2_ = bf16[64,2304]{1,0:T(8,128)(2,1)S(1)} collective-permute-done((bf16[64,2304]{1,0:T(8,128)(2,1)}, bf16[64,2304]{1,0:T(8,128)(2,1)S(1)}, u32[]{:S(2)}, u32[]{:S(2)}) %collective-permute-start.2) | collective-permute-done | bytes 294944 | tf_op jit(solution)/shard_map/ppermute | solution.py:34
  19.9 2.9 %collective-permute-start.4 = (bf16[64,2304]{1,0:T(8,128)(2,1)S(1)}, bf16[64,2304]{1,0:T(8,128)(2,1)S(1)}, u32[]{:S(2)}, u32[]{:S(2)}) collective-permute-start(bf16[64,2304]{1,0:T(8,128)(2,1)S(1)} %collective-permute-done.refs_0_), channel_id=1, source_target_pairs={{0,12},{1,13},{2,14},{3,15},{4,8},{5,9},{6,10},{7,11},{8,4},{9,5},... | collective-permute-start | bytes 884744 | tf_op jit(solution)/shard_map/ppermute | solution.py:34
  22.8 2.6 %shard_map.86.a_ref.refs_8_ = bf16[512,1024]{1,0:T(8,128)(2,1)S(1)} custom-call(bf16[64,2304]{1,0:T(8,128)(2,1)S(1)} %get-tuple-element.47.refs_0_, bf16[64,2304]{1,0:T(8,128)(2,1)S(1)} %collective-permute-done.5.refs_1_, bf16[64,2304]{1,0:T(8,128)(2,1)S(1)} %collective-permute-done.2.refs_2_, bf16[64,2304]{1,0:T(8,128)(2,1)S(1)} %collective-permute-done.6.refs_3_, ...), custom_call_target="tpu_custom_call" | custom-call | flops 2415919104 | bytes 2359296 | tf_op jit(solution)/shard_map/pallas_call | solution.py:76
  25.5 4.0 %collective-permute-done.3.refs_2_ = bf16[64,2304]{1,0:T(8,128)(2,1)S(1)} collective-permute-done((bf16[64,2304]{1,0:T(8,128)(2,1)S(1)}, bf16[64,2304]{1,0:T(8,128)(2,1)S(1)}, u32[]{:S(2)}, u32[]{:S(2)}) %collective-permute-start.3) | collective-permute-done | bytes 294944 | tf_op jit(solution)/shard_map/ppermute | solution.py:34
  32.7 2.6 %shard_map.87 = (f32[256,1280]{1,0:T(8,128)S(1)}, bf16[256,1280]{1,0:T(8,128)(2,1)S(1)}, f32[256,1024]{1,0:T(8,128)S(1)}, bf16[256,1024]{1,0:T(8,128)(2,1)S(1)}) custom-call(bf16[512,1024]{1,0:T(8,128)(2,1)S(1)} %shard_map.86.a_ref.refs_8_, bf16[1024,2304]{1,0:T(8,128)(2,1)S(1)} %get-tuple-element.51.w_ref.refs_10_), custom_call_target="tpu_custom_call" | custom-call | flops 2415919104 | bytes 3538944 | tf_op jit(solution)/shard_map/pallas_call | solution.py:76
  35.9 2.6 %shard_map.88.a_ref.refs_9_ = bf16[512,1024]{1,0:T(8,128)(2,1)S(1)} custom-call(bf16[64,2304]{1,0:T(8,128)(2,1)S(1)} %collective-permute-done.refs_0_, bf16[64,2304]{1,0:T(8,128)(2,1)S(1)} %collective-permute-done.1.refs_1_, bf16[64,2304]{1,0:T(8,128)(2,1)S(1)} %collective-permute-done.3.refs_2_, bf16[64,2304]{1,0:T(8,128)(2,1)S(1)} %collective-permute-done.4.refs_3_, ...), custom_call_target="tpu_custom_call" | custom-call | flops 2415919104 | bytes 2359296 | tf_op jit(solution)/shard_map/pallas_call | solution.py:76
  44.9 2.1 %collective-permute-start.18 = (bf16[128,1280]{1,0:T(8,128)(2,1)S(1)}, bf16[128,1280]{1,0:T(8,128)(2,1)S(1)}, u32[]{:S(2)}, u32[]{:S(2)}) collective-permute-start(bf16[128,1280]{1,0:T(8,128)(2,1)S(1)} %get-tuple-element.62), channel_id=1, source_target_pairs={{0,8},{1,3},{2,10},{3,1},{4,12},{5,7},{6,14},{7,5},{8,0},{9,11},{1... | collective-permute-start | bytes 983048 | tf_op jit(solution)/shard_map/ppermute | solution.py:34
  47.0 1.7 %collective-permute-start.19 = (bf16[128,1280]{1,0:T(8,128)(2,1)S(1)}, bf16[128,1280]{1,0:T(8,128)(2,1)S(1)}, u32[]{:S(2)}, u32[]{:S(2)}) collective-permute-start(bf16[128,1280]{1,0:T(8,128)(2,1)S(1)} %get-tuple-element.63), channel_id=1, source_target_pairs={{0,12},{1,67},{2,14},{3,65},{4,8},{5,71},{6,10},{7,69},{8,4},{9,75... | collective-permute-start | bytes 983048 | tf_op jit(solution)/shard_map/ppermute | solution.py:34
  49.3 1.7 %collective-permute-start.24 = (bf16[128,1024]{1,0:T(8,128)(2,1)S(1)}, bf16[128,1024]{1,0:T(8,128)(2,1)S(1)}, u32[]{:S(2)}, u32[]{:S(2)}) collective-permute-start(bf16[128,1024]{1,0:T(8,128)(2,1)S(1)} %get-tuple-element.71), channel_id=1, source_target_pairs={{0,12},{1,67},{2,14},{3,65},{4,8},{5,71},{6,10},{7,69},{8,4},{9,75... | collective-permute-start | bytes 786440 | tf_op jit(solution)/shard_map/ppermute | solution.py:34
  51.0 8.7 %collective-permute-done.23.refs_6_ = bf16[128,1024]{1,0:T(8,128)(2,1)S(1)} collective-permute-done((bf16[128,1024]{1,0:T(8,128)(2,1)S(1)}, bf16[128,1024]{1,0:T(8,128)(2,1)S(1)}, u32[]{:S(2)}, u32[]{:S(2)}) %collective-permute-start.23) | collective-permute-done | bytes 262176 | tf_op jit(solution)/shard_map/ppermute | solution.py:34
  59.7 4.7 %collective-permute-done.24.refs_7_ = bf16[128,1024]{1,0:T(8,128)(2,1)S(1)} collective-permute-done((bf16[128,1024]{1,0:T(8,128)(2,1)S(1)}, bf16[128,1024]{1,0:T(8,128)(2,1)S(1)}, u32[]{:S(2)}, u32[]{:S(2)}) %collective-permute-start.24) | collective-permute-done | bytes 262176 | tf_op jit(solution)/shard_map/ppermute | solution.py:34
  64.8 3.5 %collective-permute-start.26 = (bf16[32,2304]{1,0:T(8,128)(2,1)S(1)}, bf16[32,2304]{1,0:T(8,128)(2,1)S(1)}, u32[]{:S(2)}, u32[]{:S(2)}) collective-permute-start(bf16[32,2304]{1,0:T(8,128)(2,1)S(1)} %get-tuple-element.74), channel_id=1, source_target_pairs={{0,2},{1,9},{2,0},{3,11},{4,6},{5,13},{6,4},{7,15},{8,10},{9,1},{1... | collective-permute-start | bytes 442376 | tf_op jit(solution)/shard_map/ppermute | solution.py:34
  69.9 3.1 %collective-permute-done.26.g2 = bf16[32,2304]{1,0:T(8,128)(2,1)S(1)} collective-permute-done((bf16[32,2304]{1,0:T(8,128)(2,1)S(1)}, bf16[32,2304]{1,0:T(8,128)(2,1)S(1)}, u32[]{:S(2)}, u32[]{:S(2)}) %collective-permute-start.26) | collective-permute-done | bytes 147488 | tf_op jit(solution)/shard_map/ppermute | solution.py:34
  73.0 1.7 %collective-permute-done.27.g3 = bf16[32,2304]{1,0:T(8,128)(2,1)S(1)} collective-permute-done((bf16[32,2304]{1,0:T(8,128)(2,1)S(1)}, bf16[32,2304]{1,0:T(8,128)(2,1)S(1)}, u32[]{:S(2)}, u32[]{:S(2)}) %collective-permute-start.27) | collective-permute-done | bytes 147488 | tf_op jit(solution)/shard_map/ppermute | solution.py:34
  74.7 4.1 %collective-permute-start.30 = (bf16[32,2304]{1,0:T(8,128)(2,1)S(1)}, bf16[32,2304]{1,0:T(8,128)(2,1)S(1)}, u32[]{:S(2)}, u32[]{:S(2)}) collective-permute-start(bf16[32,2304]{1,0:T(8,128)(2,1)S(1)} %get-tuple-element.77), channel_id=1, source_target_pairs={{0,48},{1,49},{2,50},{3,51},{4,52},{5,53},{6,54},{7,55},{8,56},{9,... | collective-permute-start | bytes 442376 | tf_op jit(solution)/shard_map/ppermute | solution.py:34
  79.8 3.7 %collective-permute-done.30.g3 = bf16[32,2304]{1,0:T(8,128)(2,1)S(1)} collective-permute-done((bf16[32,2304]{1,0:T(8,128)(2,1)S(1)}, bf16[32,2304]{1,0:T(8,128)(2,1)S(1)}, u32[]{:S(2)}, u32[]{:S(2)}) %collective-permute-start.30) | collective-permute-done | bytes 147488 | tf_op jit(solution)/shard_map/ppermute | solution.py:34
  83.6 1.9 %collective-permute-done.29.g2 = bf16[32,2304]{1,0:T(8,128)(2,1)S(1)} collective-permute-done((bf16[32,2304]{1,0:T(8,128)(2,1)S(1)}, bf16[32,2304]{1,0:T(8,128)(2,1)S(1)}, u32[]{:S(2)}, u32[]{:S(2)}) %collective-permute-start.29) | collective-permute-done | bytes 147488 | tf_op jit(solution)/shard_map/ppermute | solution.py:34
  88.4 1.7 %collective-permute-start.32 = (bf16[32,2304]{1,0:T(8,128)(2,1)S(1)}, bf16[32,2304]{1,0:T(8,128)(2,1)S(1)}, u32[]{:S(2)}, u32[]{:S(2)}) collective-permute-start(bf16[32,2304]{1,0:T(8,128)(2,1)S(1)} %get-tuple-element.79.refs_0_), channel_id=1, source_target_pairs={{0,64},{1,5},{2,66},{3,7},{4,68},{5,1},{6,70},{7,3},{8,72},{9,13},... | collective-permute-start | bytes 442376 | tf_op jit(solution)/shard_map/ppermute | solution.py:34
  90.1 3.8 %collective-permute-done.34.refs_3_ = bf16[32,2304]{1,0:T(8,128)(2,1)S(1)} collective-permute-done((bf16[32,2304]{1,0:T(8,128)(2,1)S(1)}, bf16[32,2304]{1,0:T(8,128)(2,1)S(1)}, u32[]{:S(2)}, u32[]{:S(2)}) %collective-permute-start.34) | collective-permute-done | bytes 147488 | tf_op jit(solution)/shard_map/ppermute | solution.py:34
  95.1 1.8 %collective-permute-start.40 = (bf16[128,1280]{1,0:T(8,128)(2,1)S(1)}, bf16[128,1280]{1,0:T(8,128)(2,1)S(1)}, u32[]{:S(2)}, u32[]{:S(2)}) collective-permute-start(bf16[128,1280]{1,0:T(8,128)(2,1)S(1)} %get-tuple-element.81.refs_0_), channel_id=1, source_target_pairs={{0,12},{1,67},{2,14},{3,65},{4,8},{5,71},{6,10},{7,69},{8,4},{9,75... | collective-permute-start | bytes 983048 | tf_op jit(solution)/shard_map/ppermute | solution.py:34
  96.9 2.3 %collective-permute-start.38 = (bf16[128,1280]{1,0:T(8,128)(2,1)S(1)}, bf16[128,1280]{1,0:T(8,128)(2,1)S(1)}, u32[]{:S(2)}, u32[]{:S(2)}) collective-permute-start(bf16[128,1280]{1,0:T(8,128)(2,1)S(1)} %get-tuple-element.81.refs_0_), channel_id=1, source_target_pairs={{0,4},{1,65},{2,6},{3,67},{4,0},{5,69},{6,2},{7,71},{8,12},{9,73},... | collective-permute-start | bytes 983048 | tf_op jit(solution)/shard_map/ppermute | solution.py:34
  99.2 7.7 %collective-permute-done.40.refs_3_ = bf16[128,1280]{1,0:T(8,128)(2,1)S(1)} collective-permute-done((bf16[128,1280]{1,0:T(8,128)(2,1)S(1)}, bf16[128,1280]{1,0:T(8,128)(2,1)S(1)}, u32[]{:S(2)}, u32[]{:S(2)}) %collective-permute-start.40) | collective-permute-done | bytes 327712 | tf_op jit(solution)/shard_map/ppermute | solution.py:34
  107.8 1.8 %collective-permute-start.37 = (bf16[128,1024]{1,0:T(8,128)(2,1)S(1)}, bf16[128,1024]{1,0:T(8,128)(2,1)S(1)}, u32[]{:S(2)}, u32[]{:S(2)}) collective-permute-start(bf16[128,1024]{1,0:T(8,128)(2,1)S(1)} %get-tuple-element.83.refs_0_), channel_id=1, source_target_pairs={{0,12},{1,67},{2,14},{3,65},{4,8},{5,71},{6,10},{7,69},{8,4},{9,75... | collective-permute-start | bytes 786440 | tf_op jit(solution)/shard_map/ppermute | solution.py:34
  109.6 2.3 %collective-permute-start.35 = (bf16[128,1024]{1,0:T(8,128)(2,1)S(1)}, bf16[128,1024]{1,0:T(8,128)(2,1)S(1)}, u32[]{:S(2)}, u32[]{:S(2)}) collective-permute-start(bf16[128,1024]{1,0:T(8,128)(2,1)S(1)} %get-tuple-element.83.refs_0_), channel_id=1, source_target_pairs={{0,4},{1,65},{2,6},{3,67},{4,0},{5,69},{6,2},{7,71},{8,12},{9,73},... | collective-permute-start | bytes 786440 | tf_op jit(solution)/shard_map/ppermute | solution.py:34
  111.9 8.7 %gradients.2 = (f32[1024,1024]{1,0:T(8,128)S(1)}, bf16[1024,2304]{1,0:T(8,128)(2,1)}) custom-call(bf16[128,1280]{1,0:T(8,128)(2,1)S(1)} %get-tuple-element.81.refs_0_, bf16[128,1280]{1,0:T(8,128)(2,1)S(1)} %collective-permute-done.38.refs_1_, bf16[128,1280]{1,0:T(8,128)(2,1)S(1)} %collective-permute-done.39.refs_2_, ...), custom_call_target="tpu_custom_call" | custom-call | flops 5368709120 | bytes 16252928 | tf_op jit(solution)/shard_map/gradients/pallas_call | solution.py:373
  121.8 2.0 %collective-permute-start.31 = (f32[8,2304]{1,0:T(8,128)S(1)}, f32[8,2304]{1,0:T(8,128)S(1)}, u32[]{:S(2)}, u32[]{:S(2)}) collective-permute-start(f32[8,2304]{1,0:T(8,128)S(1)} %get-tuple-element.78), channel_id=1, source_target_pairs={{0,0},{1,8},{2,16},{3,24},{4,32},{5,40},{6,48},{7,56},{8,64},{9,72... | collective-permute-start | bytes 221192 | tf_op jit(solution)/shard_map/ppermute | solution.py:34
  123.9 10.9 %collective-permute-done.31 = f32[8,2304]{1,0:T(8,128)S(1)} collective-permute-done((f32[8,2304]{1,0:T(8,128)S(1)}, f32[8,2304]{1,0:T(8,128)S(1)}, u32[]{:S(2)}, u32[]{:S(2)}) %collective-permute-start.31) | collective-permute-done | bytes 73760 | tf_op jit(solution)/shard_map/ppermute | solution.py:34
  134.7 8.4 %gradients.3 = (bf16[1024,1024]{1,0:T(8,128)(2,1)}, bf16[1024,2304]{1,0:T(8,128)(2,1)}) custom-call(bf16[128,1024]{1,0:T(8,128)(2,1)S(1)} %get-tuple-element.83.refs_0_, bf16[128,1024]{1,0:T(8,128)(2,1)S(1)} %collective-permute-done.35.refs_1_, bf16[128,1024]{1,0:T(8,128)(2,1)S(1)} %collective-permute-done.36.refs_2_, ...), custom_call_target="tpu_custom_call", output_to_operand_aliasing={{1}: (12, {})} | custom-call | flops 4294967296 | bytes 14680064 | tf_op jit(solution)/shard_map/gradients/pallas_call | solution.py:373
  (97 shorter events, 26.2 us)
Async XLA Ops:
  0.6 13.3 %collective-permute-start.6 = (bf16[64,2304]{1,0:T(8,128)(2,1)}, bf16[64,2304]{1,0:T(8,128)(2,1)S(1)}, u32[]{:S(2)}, u32[]{:S(2)}) collective-permute-start(bf16[64,2304]{1,0:T(8,128)(2,1)} %bitcast.9), channel_id=1, source_target_pairs={{0,12},{1,13},{2,14},{3,15},{4,8},{5,9},{6,10},{7,11},{8,4},{9,5},... | collective-permute-start | bytes 884744 | tf_op jit(solution)/shard_map/ppermute | solution.py:34
  3.7 10.8 %collective-permute-start.5 = (bf16[64,2304]{1,0:T(8,128)(2,1)}, bf16[64,2304]{1,0:T(8,128)(2,1)S(1)}, u32[]{:S(2)}, u32[]{:S(2)}) collective-permute-start(bf16[64,2304]{1,0:T(8,128)(2,1)} %bitcast.10), channel_id=1, source_target_pairs={{0,4},{1,5},{2,6},{3,7},{4,0},{5,1},{6,2},{7,3},{8,12},{9,13},{10,... | collective-permute-start | bytes 884744 | tf_op jit(solution)/shard_map/ppermute | solution.py:34
  3.9 14.7 %collective-permute-start.2 = (bf16[64,2304]{1,0:T(8,128)(2,1)}, bf16[64,2304]{1,0:T(8,128)(2,1)S(1)}, u32[]{:S(2)}, u32[]{:S(2)}) collective-permute-start(bf16[64,2304]{1,0:T(8,128)(2,1)} %bitcast.11), channel_id=1, source_target_pairs={{0,8},{1,9},{2,10},{3,11},{4,12},{5,13},{6,14},{7,15},{8,0},{9,1},... | collective-permute-start | bytes 884744 | tf_op jit(solution)/shard_map/ppermute | solution.py:34
  5.4 13.1 %collective-permute-start = (bf16[64,2304]{1,0:T(8,128)(2,1)}, bf16[64,2304]{1,0:T(8,128)(2,1)S(1)}, u32[]{:S(2)}, u32[]{:S(2)}) collective-permute-start(bf16[64,2304]{1,0:T(8,128)(2,1)} %bitcast.12), channel_id=1, source_target_pairs={{0,2},{1,3},{2,0},{3,1},{4,6},{5,7},{6,4},{7,5},{8,10},{9,11},{10,... | collective-permute-start | bytes 884744 | tf_op jit(solution)/shard_map/ppermute | solution.py:34
  14.0 8.8 %collective-permute-start.10 = (bf16[64,2304]{1,0:T(8,128)(2,1)S(1)}, bf16[64,2304]{1,0:T(8,128)(2,1)S(1)}, u32[]{:S(2)}, u32[]{:S(2)}) collective-permute-start(bf16[64,2304]{1,0:T(8,128)(2,1)S(1)} %collective-permute-done.6.refs_3_), channel_id=1, source_target_pairs={{0,1},{1,0},{2,3},{3,2},{4,5},{5,4},{6,7},{7,6},{8,9},{9,8},{10,11... | collective-permute-start | bytes 884744 | tf_op jit(solution)/shard_map/ppermute | solution.py:34
  14.5 8.3 %collective-permute-start.8 = (bf16[64,2304]{1,0:T(8,128)(2,1)S(1)}, bf16[64,2304]{1,0:T(8,128)(2,1)S(1)}, u32[]{:S(2)}, u32[]{:S(2)}) collective-permute-start(bf16[64,2304]{1,0:T(8,128)(2,1)S(1)} %collective-permute-done.5.refs_1_), channel_id=1, source_target_pairs={{0,1},{1,0},{2,3},{3,2},{4,5},{5,4},{6,7},{7,6},{8,9},{9,8},{10,11... | collective-permute-start | bytes 884744 | tf_op jit(solution)/shard_map/ppermute | solution.py:34
  18.5 10.9 %collective-permute-start.3 = (bf16[64,2304]{1,0:T(8,128)(2,1)S(1)}, bf16[64,2304]{1,0:T(8,128)(2,1)S(1)}, u32[]{:S(2)}, u32[]{:S(2)}) collective-permute-start(bf16[64,2304]{1,0:T(8,128)(2,1)S(1)} %collective-permute-done.2.refs_2_), channel_id=1, source_target_pairs={{0,2},{1,3},{2,0},{3,1},{4,6},{5,7},{6,4},{7,5},{8,10},{9,11},{10,... | collective-permute-start | bytes 884744 | tf_op jit(solution)/shard_map/ppermute | solution.py:34
  19.9 10.4 %collective-permute-start.4 = (bf16[64,2304]{1,0:T(8,128)(2,1)S(1)}, bf16[64,2304]{1,0:T(8,128)(2,1)S(1)}, u32[]{:S(2)}, u32[]{:S(2)}) collective-permute-start(bf16[64,2304]{1,0:T(8,128)(2,1)S(1)} %collective-permute-done.refs_0_), channel_id=1, source_target_pairs={{0,12},{1,13},{2,14},{3,15},{4,8},{5,9},{6,10},{7,11},{8,4},{9,5},... | collective-permute-start | bytes 884744 | tf_op jit(solution)/shard_map/ppermute | solution.py:34
  22.8 8.9 %collective-permute-start.1 = (bf16[64,2304]{1,0:T(8,128)(2,1)S(1)}, bf16[64,2304]{1,0:T(8,128)(2,1)S(1)}, u32[]{:S(2)}, u32[]{:S(2)}) collective-permute-start(bf16[64,2304]{1,0:T(8,128)(2,1)S(1)} %collective-permute-done.refs_0_), channel_id=1, source_target_pairs={{0,4},{1,5},{2,6},{3,7},{4,0},{5,1},{6,2},{7,3},{8,12},{9,13},{10,... | collective-permute-start | bytes 884744 | tf_op jit(solution)/shard_map/ppermute | solution.py:34
  35.4 7.4 %collective-permute-start.15 = (bf16[256,1280]{1,0:T(8,128)(2,1)S(1)}, bf16[256,1280]{1,0:T(8,128)(2,1)S(1)}, u32[]{:S(2)}, u32[]{:S(2)}) collective-permute-start(bf16[256,1280]{1,0:T(8,128)(2,1)S(1)} %get-tuple-element.58), channel_id=1, source_target_pairs={{0,1},{1,0},{2,3},{3,2},{4,5},{5,4},{6,7},{7,6},{8,9},{9,8},{10,11... | collective-permute-start | bytes 1966088 | tf_op jit(solution)/shard_map/ppermute | solution.py:34
  42.4 6.9 %collective-permute-start.22 = (bf16[128,1024]{1,0:T(8,128)(2,1)S(1)}, bf16[128,1024]{1,0:T(8,128)(2,1)S(1)}, u32[]{:S(2)}, u32[]{:S(2)}) collective-permute-start(bf16[128,1024]{1,0:T(8,128)(2,1)S(1)} %get-tuple-element.69), channel_id=1, source_target_pairs={{0,4},{1,65},{2,6},{3,67},{4,0},{5,69},{6,2},{7,71},{8,12},{9,73},... | collective-permute-start | bytes 786440 | tf_op jit(solution)/shard_map/ppermute | solution.py:34
  44.0 20.4 %collective-permute-start.17 = (bf16[128,1280]{1,0:T(8,128)(2,1)S(1)}, bf16[128,1280]{1,0:T(8,128)(2,1)S(1)}, u32[]{:S(2)}, u32[]{:S(2)}) collective-permute-start(bf16[128,1280]{1,0:T(8,128)(2,1)S(1)} %get-tuple-element.61), channel_id=1, source_target_pairs={{0,4},{1,65},{2,6},{3,67},{4,0},{5,69},{6,2},{7,71},{8,12},{9,73},... | collective-permute-start | bytes 983048 | tf_op jit(solution)/shard_map/ppermute | solution.py:34
  44.9 19.6 %collective-permute-start.18 = (bf16[128,1280]{1,0:T(8,128)(2,1)S(1)}, bf16[128,1280]{1,0:T(8,128)(2,1)S(1)}, u32[]{:S(2)}, u32[]{:S(2)}) collective-permute-start(bf16[128,1280]{1,0:T(8,128)(2,1)S(1)} %get-tuple-element.62), channel_id=1, source_target_pairs={{0,8},{1,3},{2,10},{3,1},{4,12},{5,7},{6,14},{7,5},{8,0},{9,11},{1... | collective-permute-start | bytes 983048 | tf_op jit(solution)/shard_map/ppermute | solution.py:34
  47.0 17.4 %collective-permute-start.19 = (bf16[128,1280]{1,0:T(8,128)(2,1)S(1)}, bf16[128,1280]{1,0:T(8,128)(2,1)S(1)}, u32[]{:S(2)}, u32[]{:S(2)}) collective-permute-start(bf16[128,1280]{1,0:T(8,128)(2,1)S(1)} %get-tuple-element.63), channel_id=1, source_target_pairs={{0,12},{1,67},{2,14},{3,65},{4,8},{5,71},{6,10},{7,69},{8,4},{9,75... | collective-permute-start | bytes 983048 | tf_op jit(solution)/shard_map/ppermute | solution.py:34
  48.7 11.0 %collective-permute-start.23 = (bf16[128,1024]{1,0:T(8,128)(2,1)S(1)}, bf16[128,1024]{1,0:T(8,128)(2,1)S(1)}, u32[]{:S(2)}, u32[]{:S(2)}) collective-permute-start(bf16[128,1024]{1,0:T(8,128)(2,1)S(1)} %get-tuple-element.70), channel_id=1, source_target_pairs={{0,8},{1,3},{2,10},{3,1},{4,12},{5,7},{6,14},{7,5},{8,0},{9,11},{1... | collective-permute-start | bytes 786440 | tf_op jit(solution)/shard_map/ppermute | solution.py:34
  49.3 15.1 %collective-permute-start.24 = (bf16[128,1024]{1,0:T(8,128)(2,1)S(1)}, bf16[128,1024]{1,0:T(8,128)(2,1)S(1)}, u32[]{:S(2)}, u32[]{:S(2)}) collective-permute-start(bf16[128,1024]{1,0:T(8,128)(2,1)S(1)} %get-tuple-element.71), channel_id=1, source_target_pairs={{0,12},{1,67},{2,14},{3,65},{4,8},{5,71},{6,10},{7,69},{8,4},{9,75... | collective-permute-start | bytes 786440 | tf_op jit(solution)/shard_map/ppermute | solution.py:34
  64.8 8.2 %collective-permute-start.26 = (bf16[32,2304]{1,0:T(8,128)(2,1)S(1)}, bf16[32,2304]{1,0:T(8,128)(2,1)S(1)}, u32[]{:S(2)}, u32[]{:S(2)}) collective-permute-start(bf16[32,2304]{1,0:T(8,128)(2,1)S(1)} %get-tuple-element.74), channel_id=1, source_target_pairs={{0,2},{1,9},{2,0},{3,11},{4,6},{5,13},{6,4},{7,15},{8,10},{9,1},{1... | collective-permute-start | bytes 442376 | tf_op jit(solution)/shard_map/ppermute | solution.py:34
  74.7 8.8 %collective-permute-start.30 = (bf16[32,2304]{1,0:T(8,128)(2,1)S(1)}, bf16[32,2304]{1,0:T(8,128)(2,1)S(1)}, u32[]{:S(2)}, u32[]{:S(2)}) collective-permute-start(bf16[32,2304]{1,0:T(8,128)(2,1)S(1)} %get-tuple-element.77), channel_id=1, source_target_pairs={{0,48},{1,49},{2,50},{3,51},{4,52},{5,53},{6,54},{7,55},{8,56},{9,... | collective-permute-start | bytes 442376 | tf_op jit(solution)/shard_map/ppermute | solution.py:34
  85.9 8.0 %collective-permute-start.34 = (bf16[32,2304]{1,0:T(8,128)(2,1)S(1)}, bf16[32,2304]{1,0:T(8,128)(2,1)S(1)}, u32[]{:S(2)}, u32[]{:S(2)}) collective-permute-start(bf16[32,2304]{1,0:T(8,128)(2,1)S(1)} %get-tuple-element.79.refs_0_), channel_id=1, source_target_pairs={{0,66},{1,13},{2,64},{3,15},{4,70},{5,9},{6,68},{7,11},{8,74},{9,5... | collective-permute-start | bytes 442376 | tf_op jit(solution)/shard_map/ppermute | solution.py:34
  87.1 6.8 %collective-permute-start.33 = (bf16[32,2304]{1,0:T(8,128)(2,1)S(1)}, bf16[32,2304]{1,0:T(8,128)(2,1)S(1)}, u32[]{:S(2)}, u32[]{:S(2)}) collective-permute-start(bf16[32,2304]{1,0:T(8,128)(2,1)S(1)} %get-tuple-element.79.refs_0_), channel_id=1, source_target_pairs={{0,2},{1,9},{2,0},{3,11},{4,6},{5,13},{6,4},{7,15},{8,10},{9,1},{1... | collective-permute-start | bytes 442376 | tf_op jit(solution)/shard_map/ppermute | solution.py:34
  95.1 11.9 %collective-permute-start.40 = (bf16[128,1280]{1,0:T(8,128)(2,1)S(1)}, bf16[128,1280]{1,0:T(8,128)(2,1)S(1)}, u32[]{:S(2)}, u32[]{:S(2)}) collective-permute-start(bf16[128,1280]{1,0:T(8,128)(2,1)S(1)} %get-tuple-element.81.refs_0_), channel_id=1, source_target_pairs={{0,12},{1,67},{2,14},{3,65},{4,8},{5,71},{6,10},{7,69},{8,4},{9,75... | collective-permute-start | bytes 983048 | tf_op jit(solution)/shard_map/ppermute | solution.py:34
  96.9 10.0 %collective-permute-start.39 = (bf16[128,1280]{1,0:T(8,128)(2,1)S(1)}, bf16[128,1280]{1,0:T(8,128)(2,1)S(1)}, u32[]{:S(2)}, u32[]{:S(2)}) collective-permute-start(bf16[128,1280]{1,0:T(8,128)(2,1)S(1)} %get-tuple-element.81.refs_0_), channel_id=1, source_target_pairs={{0,8},{1,3},{2,10},{3,1},{4,12},{5,7},{6,14},{7,5},{8,0},{9,11},{1... | collective-permute-start | bytes 983048 | tf_op jit(solution)/shard_map/ppermute | solution.py:34
  96.9 10.9 %collective-permute-start.38 = (bf16[128,1280]{1,0:T(8,128)(2,1)S(1)}, bf16[128,1280]{1,0:T(8,128)(2,1)S(1)}, u32[]{:S(2)}, u32[]{:S(2)}) collective-permute-start(bf16[128,1280]{1,0:T(8,128)(2,1)S(1)} %get-tuple-element.81.refs_0_), channel_id=1, source_target_pairs={{0,4},{1,65},{2,6},{3,67},{4,0},{5,69},{6,2},{7,71},{8,12},{9,73},... | collective-permute-start | bytes 983048 | tf_op jit(solution)/shard_map/ppermute | solution.py:34
  99.2 10.4 %collective-permute-start.41 = (bf16[128,1280]{1,0:T(8,128)(2,1)S(1)}, bf16[128,1280]{1,0:T(8,128)(2,1)S(1)}, u32[]{:S(2)}, u32[]{:S(2)}) collective-permute-start(bf16[128,1280]{1,0:T(8,128)(2,1)S(1)} %get-tuple-element.81.refs_0_), channel_id=1, source_target_pairs={{0,1},{1,0},{2,3},{3,2},{4,5},{5,4},{6,7},{7,6},{8,9},{9,8},{10,11... | collective-permute-start | bytes 983048 | tf_op jit(solution)/shard_map/ppermute | solution.py:34
  107.8 12.9 %collective-permute-start.37 = (bf16[128,1024]{1,0:T(8,128)(2,1)S(1)}, bf16[128,1024]{1,0:T(8,128)(2,1)S(1)}, u32[]{:S(2)}, u32[]{:S(2)}) collective-permute-start(bf16[128,1024]{1,0:T(8,128)(2,1)S(1)} %get-tuple-element.83.refs_0_), channel_id=1, source_target_pairs={{0,12},{1,67},{2,14},{3,65},{4,8},{5,71},{6,10},{7,69},{8,4},{9,75... | collective-permute-start | bytes 786440 | tf_op jit(solution)/shard_map/ppermute | solution.py:34
  109.6 11.1 %collective-permute-start.36 = (bf16[128,1024]{1,0:T(8,128)(2,1)S(1)}, bf16[128,1024]{1,0:T(8,128)(2,1)S(1)}, u32[]{:S(2)}, u32[]{:S(2)}) collective-permute-start(bf16[128,1024]{1,0:T(8,128)(2,1)S(1)} %get-tuple-element.83.refs_0_), channel_id=1, source_target_pairs={{0,8},{1,3},{2,10},{3,1},{4,12},{5,7},{6,14},{7,5},{8,0},{9,11},{1... | collective-permute-start | bytes 786440 | tf_op jit(solution)/shard_map/ppermute | solution.py:34
  109.6 11.1 %collective-permute-start.35 = (bf16[128,1024]{1,0:T(8,128)(2,1)S(1)}, bf16[128,1024]{1,0:T(8,128)(2,1)S(1)}, u32[]{:S(2)}, u32[]{:S(2)}) collective-permute-start(bf16[128,1024]{1,0:T(8,128)(2,1)S(1)} %get-tuple-element.83.refs_0_), channel_id=1, source_target_pairs={{0,4},{1,65},{2,6},{3,67},{4,0},{5,69},{6,2},{7,71},{8,12},{9,73},... | collective-permute-start | bytes 786440 | tf_op jit(solution)/shard_map/ppermute | solution.py:34
  120.7 14.0 %collective-permute-start.45 = (bf16[128,1024]{1,0:T(8,128)(2,1)S(1)}, bf16[128,1024]{1,0:T(8,128)(2,1)S(1)}, u32[]{:S(2)}, u32[]{:S(2)}) collective-permute-start(bf16[128,1024]{1,0:T(8,128)(2,1)S(1)} %get-tuple-element.83.refs_0_), channel_id=1, source_target_pairs={{0,1},{1,0},{2,3},{3,2},{4,5},{5,4},{6,7},{7,6},{8,9},{9,8},{10,11... | collective-permute-start | bytes 786440 | tf_op jit(solution)/shard_map/ppermute | solution.py:34
  120.8 13.9 %collective-permute-start.46 = (bf16[128,1024]{1,0:T(8,128)(2,1)S(1)}, bf16[128,1024]{1,0:T(8,128)(2,1)S(1)}, u32[]{:S(2)}, u32[]{:S(2)}) collective-permute-start(bf16[128,1024]{1,0:T(8,128)(2,1)S(1)} %collective-permute-done.35.refs_1_), channel_id=1, source_target_pairs={{0,1},{1,0},{2,3},{3,2},{4,5},{5,4},{6,7},{7,6},{8,9},{9,8},{10,11... | collective-permute-start | bytes 786440 | tf_op jit(solution)/shard_map/ppermute | solution.py:34
  121.3 13.4 %collective-permute-start.47 = (bf16[128,1024]{1,0:T(8,128)(2,1)S(1)}, bf16[128,1024]{1,0:T(8,128)(2,1)S(1)}, u32[]{:S(2)}, u32[]{:S(2)}) collective-permute-start(bf16[128,1024]{1,0:T(8,128)(2,1)S(1)} %collective-permute-done.36.refs_2_), channel_id=1, source_target_pairs={{0,1},{1,0},{2,3},{3,2},{4,5},{5,4},{6,7},{7,6},{8,9},{9,8},{10,11... | collective-permute-start | bytes 786440 | tf_op jit(solution)/shard_map/ppermute | solution.py:34
  121.4 13.3 %collective-permute-start.48 = (bf16[128,1024]{1,0:T(8,128)(2,1)S(1)}, bf16[128,1024]{1,0:T(8,128)(2,1)S(1)}, u32[]{:S(2)}, u32[]{:S(2)}) collective-permute-start(bf16[128,1024]{1,0:T(8,128)(2,1)S(1)} %collective-permute-done.37.refs_3_), channel_id=1, source_target_pairs={{0,1},{1,0},{2,3},{3,2},{4,5},{5,4},{6,7},{7,6},{8,9},{9,8},{10,11... | collective-permute-start | bytes 786440 | tf_op jit(solution)/shard_map/ppermute | solution.py:34
  121.8 12.9 %collective-permute-start.31 = (f32[8,2304]{1,0:T(8,128)S(1)}, f32[8,2304]{1,0:T(8,128)S(1)}, u32[]{:S(2)}, u32[]{:S(2)}) collective-permute-start(f32[8,2304]{1,0:T(8,128)S(1)} %get-tuple-element.78), channel_id=1, source_target_pairs={{0,0},{1,8},{2,16},{3,24},{4,32},{5,40},{6,48},{7,56},{8,64},{9,72... | collective-permute-start | bytes 221192 | tf_op jit(solution)/shard_map/ppermute | solution.py:34
  (24 other events, 209.5 us)
